TPU v7x, 128 devices: a whole 4x4x4 slice. The times are simulated.
128 devices in a mesh: section: 32 (over y, z, core), tensor: 4 (over x).
Axes of the slice: x: 4, y: 4, z: 4, core: 2. Of those that a mesh axis runs over, the one named last changes fastest.
Arguments:
- section_input: bfloat16 [32, 512, 4096], P('section', 'tensor'), may hold values from -6 to 6
- history: bfloat16 [32, 7, 512, 4096], P('section', None, 'tensor'), may hold values from -6 to 6
- query_weight: bfloat16 [32, 4096, 3072], P('section', None, 'tensor'), may hold values from -0.4 to 0.4
- key_weight: bfloat16 [32, 4096, 512], P('section', None, 'tensor'), may hold values from -0.4 to 0.4
- value_weight: bfloat16 [32, 4096, 512], P('section', None, 'tensor'), may hold values from -0.09375 to 0.09375
- output_weight: bfloat16 [32, 3072, 4096], P('section', 'tensor'), may hold values from -0.5 to 0.5
- mix_weights: float32 [32, 8], replicated, may hold values from 0.2 to 0.6
Outputs:
- next_input: bfloat16 [32, 512, 4096], P('section', 'tensor')
All inputs are finite; a program needn't handle non-finite values.
Results may differ from a plain program's by a relative error of at most 0.013.
The roundings to bfloat16 on the way count: a program that leaves them out, or rounds other values in their place, can miss the bound.
Values may be sent and summed in bfloat16 or wider, within the bound.
No kernel may reach another device: no remote copies, remote signals or barrier semaphores. Data moves between devices by JAX's collectives and lax.ppermute only.
A program may use at most 128 MiB of HBM per device.

v0:
```python
import math
import jax
import jax.numpy as jnp
from jax import lax
from jax.sharding import PartitionSpec as P

HEAD_DIM = 64
DILATION_STRIDE = 4


def passed_along(value, axis, steps):
    count = lax.axis_size(axis)
    first, last = (max(0, -steps), min(count, count - steps))
    return lax.ppermute(value, axis, [(source, source + steps) for source in range(first, last)])


def from_behind(block, axis, distance):
    devices = range(lax.axis_size(axis))
    route = [((i - distance) % len(devices), i) for i in devices]
    return lax.ppermute(block, axis, route)


def normalize(token_rows):
    values = token_rows.astype(jnp.float32)
    inv_scale = lax.rsqrt(jnp.mean(values * values, axis=-1, keepdims=True) + 1e-05)
    return (values * inv_scale).astype(jnp.bfloat16)


def table_row(table, wanted):
    one_hot = (jnp.arange(table.shape[0], dtype=jnp.int32) == wanted).astype(jnp.float32)
    return jnp.sum(one_hot[:, None] * table, axis=0)


def attend(query_rows, key_rows, value_rows, first_row):
    scores = jnp.einsum(
        "tgjd,sgd->gjts", query_rows, key_rows, preferred_element_type=jnp.float32
    ) / math.sqrt(HEAD_DIM)
    row_positions = first_row + jnp.arange(query_rows.shape[0], dtype=jnp.int32)
    key_positions = jnp.arange(key_rows.shape[0], dtype=jnp.int32)
    scores = jnp.where(row_positions[:, None] >= key_positions[None, :], scores, -1e30)
    softmax_weights = jax.nn.softmax(scores, axis=-1).astype(jnp.bfloat16)
    heads_out = jnp.einsum(
        "gjts,sgd->tgjd", softmax_weights, value_rows, preferred_element_type=jnp.float32
    )
    return heads_out.astype(jnp.bfloat16)


def on_device(
    section_input, history, query_weight, key_weight, value_weight, output_weight, mix_weights
):
    token_rows = section_input[0]
    current_section = lax.axis_index("section")
    slots = history.shape[1]
    self_coefficient = table_row(mix_weights, current_section)
    history_sum = jnp.zeros(token_rows.shape, jnp.float32)
    for history_slot in range(1, slots + 1):
        received_block = passed_along(
            history[0, history_slot - 1], "section", DILATION_STRIDE * history_slot
        )
        factor = jnp.where(
            current_section >= DILATION_STRIDE * history_slot,
            self_coefficient[history_slot],
            jnp.float32(0.0),
        )
        history_sum = history_sum + factor * received_block.astype(jnp.float32)
    normed = normalize(token_rows)
    query_local = query_weight[0]
    key_local = key_weight[0]
    value_local = value_weight[0]
    row_piece = lax.all_gather(normed, "tensor", axis=0, tiled=True)
    query_part = jnp.dot(row_piece, query_local, preferred_element_type=jnp.float32).astype(
        jnp.bfloat16
    )
    key_part = jnp.dot(row_piece, key_local, preferred_element_type=jnp.float32).astype(
        jnp.bfloat16
    )
    value_part = jnp.dot(row_piece, value_local, preferred_element_type=jnp.float32).astype(
        jnp.bfloat16
    )
    projected = jnp.concatenate([query_part, key_part, value_part], axis=1)
    query_width = query_local.shape[1]
    kv_width = key_local.shape[1]
    seq_len = projected.shape[0]
    groups = kv_width // HEAD_DIM
    per_group = query_width // kv_width
    query_rows = projected[:, :query_width].reshape(seq_len, groups, per_group, HEAD_DIM)
    key_rows = projected[:, query_width : query_width + kv_width].reshape(seq_len, groups, HEAD_DIM)
    value_rows = projected[:, query_width + kv_width :].reshape(seq_len, groups, HEAD_DIM)
    block_rows = 512
    block_count = seq_len // block_rows
    blocked = query_rows.reshape(block_count, block_rows, groups, per_group, HEAD_DIM)
    starts = jnp.arange(block_count, dtype=jnp.int32) * block_rows
    attended = lax.map(
        lambda paired: attend(paired[0], key_rows, value_rows, paired[1]), (blocked, starts)
    )
    heads_out = attended.reshape(seq_len, query_width)
    output_local = output_weight[0]
    row_piece = heads_out
    partial_term = jnp.dot(row_piece, output_local, preferred_element_type=jnp.float32).astype(
        jnp.bfloat16
    )
    attention_sum = lax.psum_scatter(
        lax.optimization_barrier(partial_term).astype(jnp.float32).astype(jnp.bfloat16),
        "tensor",
        scatter_dimension=0,
        tiled=True,
    ).astype(jnp.float32)
    block_out = (token_rows.astype(jnp.float32) + attention_sum).astype(jnp.bfloat16)
    mixed = (self_coefficient[0] * block_out.astype(jnp.float32) + history_sum).astype(jnp.bfloat16)
    forwarded = from_behind(mixed, "section", 1)
    return forwarded[None]


def solution(mesh):
    placed = (
        P("section", "tensor", None),
        P("section", None, "tensor", None),
        P("section", None, "tensor"),
        P("section", None, "tensor"),
        P("section", None, "tensor"),
        P("section", "tensor", None),
        P(),
    )
    return jax.shard_map(
        on_device,
        mesh=mesh,
        in_specs=placed,
        out_specs=P("section", "tensor", None),
        check_vma=False,
    )
```

profile of v0, /device:TPU:0, one launch (start us, length us, event | category | flops | bytes accessed | tf_op | source)
XLA Modules:
  0.0 245.2 jit_solution(5167761586907813160)
XLA Ops:
  6.5 1.6 fusion.13
  8.2 2.5 %fusion.14 = bf16[128,4096]{1,0:T(8,128)(2,1)} fusion(bf16[1,128,4096]{2,1,0:T(8,128)(2,1)} %param.7, f32[128]{0:T(128)S(1)} %add_rsqrt_fusion), kind=kLoop, calls=%fused_computation.18 | loop fusion | flops 1572864 | bytes 2097664 | tf_op jit(solution)/shard_map/convert_element_type | solution.py:26
  10.8 50.7 %all-gather.2.cloned.1.call-done = bf16[512,4096]{1,0:T(8,128)(2,1)} async-done(((bf16[128,4096]{1,0:T(8,128)(2,1)}), bf16[512,4096]{1,0:T(8,128)(2,1)}) %all-gather.2.cloned.1.call-update) | async-done | bytes 4194320 | tf_op jit(solution)/shard_map/all_gather | solution.py:70
  61.5 7.5 %fusion.19 = bf16[512,768]{1,0:T(8,128)(2,1)S(1)} fusion(bf16[512,4096]{1,0:T(8,128)(2,1)} %all-gather.2.cloned.1.call-done, bf16[1,4096,768]{2,1,0:T(8,128)(2,1)} %param.9), kind=kOutput, calls=%fused_computation.23 | convolution fusion | flops 3221618688 | bytes 11272192 | tf_op jit(solution)/shard_map/dot_general | solution.py:71
  69.2 3.7 %convolution_convert_fusion = bf16[512,128]{0,1:T(8,128)(2,1)S(1)} fusion(bf16[512,4096]{1,0:T(8,128)(2,1)} %all-gather.2.cloned.1.call-done, bf16[1,4096,128]{2,1,0:T(8,128)(2,1)S(1)} %copy-done), kind=kOutput, calls=%fused_computation.24 | convolution fusion | flops 536936448 | bytes 5373952 | tf_op jit(solution)/shard_map/dot_general | solution.py:74
  72.9 7.3 %fusion.27 = (f32[2,6,512]{2,1,0:T(8,128)S(1)}, f32[2,6,512,512]{2,3,1,0:T(8,128)}) fusion(pred[512,512]{0,1:T(8,128)(4,1)S(1)} %iota_compare_fusion, bf16[512,2,64,1]{0,2,3,1:T(8,128)(2,1)S(1)} %bitcast.80, bf16[512,2,6,64]{0,3,2,1:T(8,128)(2,1)S(1)} %bitcast.79), kind=kOutput, calls=%fused_computation.42 | convolution fusion | flops 415236608 | bytes 13787136 | tf_op jit(solution)/shard_map/while/body/eval_jaxpr/sub | solution.py:41
  80.2 3.8 %convolution_convert_fusion.1 = bf16[512,128]{0,1:T(8,128)(2,1)S(1)} fusion(bf16[512,4096]{1,0:T(8,128)(2,1)} %all-gather.2.cloned.1.call-done, bf16[1,4096,128]{2,1,0:T(8,128)(2,1)S(1)} %copy-done.2), kind=kOutput, calls=%fused_computation.25 | convolution fusion | flops 536936448 | bytes 5373952 | tf_op jit(solution)/shard_map/dot_general | solution.py:77
  84.1 6.0 %fusion.18 = bf16[2,64,6,512]{3,1,2,0:T(8,128)(2,1)S(1)} fusion(bf16[512,2,64,1]{0,2,3,1:T(8,128)(2,1)S(1)} %bitcast.81, f32[2,6,512,512]{2,3,1,0:T(8,128)} %get-tuple-element.36, f32[2,6,512]{2,1,0:T(8,128)S(1)} %get-tuple-element.35), kind=kOutput, calls=%fused_computation.22 | convolution fusion | flops 409337856 | bytes 13524992 | tf_op jit(solution)/shard_map/while/body/eval_jaxpr/gjts,sgd->tgjd/dot_general | solution.py:42
  90.1 5.2 %fusion.10 = bf16[512,4096]{1,0:T(8,128)(2,1)} fusion(bf16[512,768]{0,1:T(8,128)(2,1)S(1)} %bitcast.84, bf16[1,768,4096]{2,1,0:T(8,128)(2,1)S(1)} %bitcast.83), kind=kOutput, calls=%fused_computation.13 | convolution fusion | flops 3223322624 | bytes 11272192 | tf_op jit(solution)/shard_map/dot_general | solution.py:99
  95.4 5.6 %slice_bitcast_fusion.6 = (bf16[128,4096]{1,0:T(8,128)(2,1)S(1)}, bf16[128,4096]{1,0:T(8,128)(2,1)}, bf16[128,4096]{1,0:T(8,128)(2,1)}, bf16[128,4096]{1,0:T(8,1...) fusion(bf16[1,7,128,4096]{3,2,1,0:T(8,128)(2,1)} %param.8), kind=kLoop, calls=%fused_computation.34 | loop fusion | bytes 14680064 | tf_op jit(solution)/shard_map/squeeze | solution.py:58
  100.9 5.1 %collective-permute-start = (bf16[128,4096]{1,0:T(8,128)(2,1)S(1)}, bf16[128,4096]{1,0:T(8,128)(2,1)S(1)}, u32[]{:S(2)}, u32[]{:S(2)}) collective-permute-start(bf16[128,4096]{1,0:T(8,128)(2,1)S(1)} %get-tuple-element.13), channel_id=1, source_target_pairs={{0,16},{4,20},{8,24},{12,28},{16,32},{20,36},{24,40},{28,44},{32,4... | collective-permute-start | bytes 3145736 | tf_op jit(solution)/shard_map/ppermute | solution.py:14
  106.1 3.4 %collective-permute-start.1 = (bf16[128,4096]{1,0:T(8,128)(2,1)S(1)}, bf16[128,4096]{1,0:T(8,128)(2,1)S(1)}, u32[]{:S(2)}, u32[]{:S(2)}) collective-permute-start(bf16[128,4096]{1,0:T(8,128)(2,1)S(1)} %get-tuple-element.24), channel_id=1, source_target_pairs={{0,32},{4,36},{8,40},{12,44},{16,48},{20,52},{24,56},{28,60},{32,6... | collective-permute-start | bytes 3145736 | tf_op jit(solution)/shard_map/ppermute | solution.py:14
  109.5 4.7 %collective-permute-start.2 = (bf16[128,4096]{1,0:T(8,128)(2,1)}, bf16[128,4096]{1,0:T(8,128)(2,1)}, u32[]{:S(2)}, u32[]{:S(2)}) collective-permute-start(bf16[128,4096]{1,0:T(8,128)(2,1)} %get-tuple-element.22), channel_id=1, source_target_pairs={{0,48},{4,52},{8,56},{12,60},{16,64},{20,68},{24,72},{28,76},{32,8... | collective-permute-start | bytes 3145736 | tf_op jit(solution)/shard_map/ppermute | solution.py:14
  114.2 2.8 %collective-permute-start.3 = (bf16[128,4096]{1,0:T(8,128)(2,1)}, bf16[128,4096]{1,0:T(8,128)(2,1)}, u32[]{:S(2)}, u32[]{:S(2)}) collective-permute-start(bf16[128,4096]{1,0:T(8,128)(2,1)} %get-tuple-element.20), channel_id=1, source_target_pairs={{0,64},{4,68},{8,72},{12,76},{16,80},{20,84},{24,88},{28,92},{32,9... | collective-permute-start | bytes 3145736 | tf_op jit(solution)/shard_map/ppermute | solution.py:14
  117.0 2.3 collective-permute-start.4
  119.3 8.9 %collective-permute-done = bf16[128,4096]{1,0:T(8,128)(2,1)S(1)} collective-permute-done((bf16[128,4096]{1,0:T(8,128)(2,1)S(1)}, bf16[128,4096]{1,0:T(8,128)(2,1)S(1)}, u32[]{:S(2)}, u32[]{:S(2)}) %collective-permute-start) | collective-permute-done | bytes 1048608 | tf_op jit(solution)/shard_map/ppermute | solution.py:14
  128.2 29.9 %collective-permute-start.5 = (bf16[128,4096]{1,0:T(8,128)(2,1)}, bf16[128,4096]{1,0:T(8,128)(2,1)}, u32[]{:S(2)}, u32[]{:S(2)}) collective-permute-start(bf16[128,4096]{1,0:T(8,128)(2,1)} %get-tuple-element.26), channel_id=1, source_target_pairs={{0,96},{4,100},{8,104},{12,108},{16,112},{20,116},{24,120},{28,124... | collective-permute-start | bytes 3145736 | tf_op jit(solution)/shard_map/ppermute | solution.py:14
  158.2 20.5 %collective-permute-start.6 = (bf16[128,4096]{1,0:T(8,128)(2,1)S(1)}, bf16[128,4096]{1,0:T(8,128)(2,1)}, u32[]{:S(2)}, u32[]{:S(2)}) collective-permute-start(bf16[128,4096]{1,0:T(8,128)(2,1)S(1)} %get-tuple-element.25), channel_id=1, source_target_pairs={{0,112},{4,116},{8,120},{12,124},{1,113},{5,117},{9,121},{13,125},... | collective-permute-start | bytes 3145736 | tf_op jit(solution)/shard_map/ppermute | solution.py:14
  178.8 0.7 fusion.26
  183.8 15.1 %collective-permute-done.4 = bf16[128,4096]{1,0:T(8,128)(2,1)} collective-permute-done((bf16[128,4096]{1,0:T(8,128)(2,1)}, bf16[128,4096]{1,0:T(8,128)(2,1)}, u32[]{:S(2)}, u32[]{:S(2)}) %collective-permute-start.4) | collective-permute-done | bytes 1048608 | tf_op jit(solution)/shard_map/ppermute | solution.py:14
  198.9 11.4 %collective-permute-done.6 = bf16[128,4096]{1,0:T(8,128)(2,1)} collective-permute-done((bf16[128,4096]{1,0:T(8,128)(2,1)S(1)}, bf16[128,4096]{1,0:T(8,128)(2,1)}, u32[]{:S(2)}, u32[]{:S(2)}) %collective-permute-start.6) | collective-permute-done | bytes 1048608 | tf_op jit(solution)/shard_map/ppermute | solution.py:14
  210.3 5.8 %add_convert_fusion = bf16[128,4096]{1,0:T(8,128)(2,1)S(1)} fusion(bf16[128,4096]{1,0:T(8,128)(2,1)} %collective-permute-done.6, bf16[128,4096]{1,0:T(8,128)(2,1)} %collective-permute-done.5, bf16[128,4096]{1,0:T(8,128)(2,1)} %collective-permute-done.4, bf16[128,4096]{1,0:T(8,128)(2,1)} %collective-permute-done.3, ...), kind=kLoop, calls=%fused_computation.20 | loop fusion | flops 14680064 | bytes 10485792 | tf_op jit(solution)/shard_map/convert_element_type | solution.py:109
  216.2 21.2 %collective-permute-done.7 = bf16[128,4096]{1,0:T(8,128)(2,1)S(1)} collective-permute-done((bf16[128,4096]{1,0:T(8,128)(2,1)S(1)}, bf16[128,4096]{1,0:T(8,128)(2,1)S(1)}, u32[]{:S(2)}, u32[]{:S(2)}) %collective-permute-start.7) | collective-permute-done | bytes 1048608 | tf_op jit(solution)/shard_map/ppermute | solution.py:20
  237.4 1.0 copy.16
  (32 shorter events, 0.7 us)
Async XLA Ops:
  6.5 62.7 %copy-start = (bf16[1,4096,128]{2,1,0:T(8,128)(2,1)S(1)}, bf16[1,4096,128]{2,1,0:T(8,128)(2,1)}, u32[]{:S(2)}) copy-start(bf16[1,4096,128]{2,1,0:T(8,128)(2,1)} %param.10) | copy-start | bytes 3145732
  6.5 54.9 %all-gather.2.cloned.1.call-start = ((), (), s32[]{:S(2)}) async-start(), calls=%async_computation.1 | async-start | bytes 5242880 | tf_op jit(solution)/shard_map/all_gather | solution.py:70
  10.6 199.6 %reduce-scatter.2.cloned.1.call-start = ((), (), s32[]{:S(2)}) async-start(), calls=%async_computation.2 | async-start | bytes 5242880 | tf_op jit(solution)/shard_map/reduce_scatter | solution.py:102
  72.9 7.3 %copy-start.2 = (bf16[1,4096,128]{2,1,0:T(8,128)(2,1)S(1)}, bf16[1,4096,128]{2,1,0:T(8,128)(2,1)}, u32[]{:S(2)}) copy-start(bf16[1,4096,128]{2,1,0:T(8,128)(2,1)} %param.11) | copy-start | bytes 3145732
  80.2 9.9 %slice-start = ((s8[6291456]{0:T(1024)(128)(4,1)}), s8[4194304]{0:T(1024)(128)(4,1)S(1)}, s32[]{:S(2)}) async-start(s8[6291456]{0:T(1024)(128)(4,1)} %bitcast.82), calls=%async_computation.3 | async-start | bytes 8388608
  84.1 6.0 %slice-start.1 = ((s8[6291456]{0:T(1024)(128)(4,1)}), s8[2097152]{0:T(1024)(128)(4,1)S(1)}, s32[]{:S(2)}) async-start(s8[6291456]{0:T(1024)(128)(4,1)} %bitcast.82), calls=%async_computation.4 | async-start | bytes 4194304
  95.3 83.4 %copy-start.5 = (f32[32,8]{0,1:T(8,128)S(1)}, f32[32,8]{0,1:T(8,128)}, u32[]{:S(2)}) copy-start(f32[32,8]{0,1:T(8,128)} %param.13) | copy-start | bytes 3076
  95.3 114.9 %copy-start.1 = (bf16[1,128,4096]{2,1,0:T(8,128)(2,1)S(1)}, bf16[1,128,4096]{2,1,0:T(8,128)(2,1)}, u32[]{:S(2)}) copy-start(bf16[1,128,4096]{2,1,0:T(8,128)(2,1)} %param.7) | copy-start | bytes 3145732
  100.9 27.3 %collective-permute-start = (bf16[128,4096]{1,0:T(8,128)(2,1)S(1)}, bf16[128,4096]{1,0:T(8,128)(2,1)S(1)}, u32[]{:S(2)}, u32[]{:S(2)}) collective-permute-start(bf16[128,4096]{1,0:T(8,128)(2,1)S(1)} %get-tuple-element.13), channel_id=1, source_target_pairs={{0,16},{4,20},{8,24},{12,28},{16,32},{20,36},{24,40},{28,44},{32,4... | collective-permute-start | bytes 3145736 | tf_op jit(solution)/shard_map/ppermute | solution.py:14
  106.1 52.1 %collective-permute-start.1 = (bf16[128,4096]{1,0:T(8,128)(2,1)S(1)}, bf16[128,4096]{1,0:T(8,128)(2,1)S(1)}, u32[]{:S(2)}, u32[]{:S(2)}) collective-permute-start(bf16[128,4096]{1,0:T(8,128)(2,1)S(1)} %get-tuple-element.24), channel_id=1, source_target_pairs={{0,32},{4,36},{8,40},{12,44},{16,48},{20,52},{24,56},{28,60},{32,6... | collective-permute-start | bytes 3145736 | tf_op jit(solution)/shard_map/ppermute | solution.py:14
  109.5 74.3 %collective-permute-start.2 = (bf16[128,4096]{1,0:T(8,128)(2,1)}, bf16[128,4096]{1,0:T(8,128)(2,1)}, u32[]{:S(2)}, u32[]{:S(2)}) collective-permute-start(bf16[128,4096]{1,0:T(8,128)(2,1)} %get-tuple-element.22), channel_id=1, source_target_pairs={{0,48},{4,52},{8,56},{12,60},{16,64},{20,68},{24,72},{28,76},{32,8... | collective-permute-start | bytes 3145736 | tf_op jit(solution)/shard_map/ppermute | solution.py:14
  114.2 69.6 %collective-permute-start.3 = (bf16[128,4096]{1,0:T(8,128)(2,1)}, bf16[128,4096]{1,0:T(8,128)(2,1)}, u32[]{:S(2)}, u32[]{:S(2)}) collective-permute-start(bf16[128,4096]{1,0:T(8,128)(2,1)} %get-tuple-element.20), channel_id=1, source_target_pairs={{0,64},{4,68},{8,72},{12,76},{16,80},{20,84},{24,88},{28,92},{32,9... | collective-permute-start | bytes 3145736 | tf_op jit(solution)/shard_map/ppermute | solution.py:14
  117.0 81.9 %collective-permute-start.4 = (bf16[128,4096]{1,0:T(8,128)(2,1)}, bf16[128,4096]{1,0:T(8,128)(2,1)}, u32[]{:S(2)}, u32[]{:S(2)}) collective-permute-start(bf16[128,4096]{1,0:T(8,128)(2,1)} %get-tuple-element.14), channel_id=1, source_target_pairs={{0,80},{4,84},{8,88},{12,92},{16,96},{20,100},{24,104},{28,108},{3... | collective-permute-start | bytes 3145736 | tf_op jit(solution)/shard_map/ppermute | solution.py:14
  128.2 50.5 %copy-start.3 = (bf16[128,4096]{1,0:T(8,128)(2,1)}, bf16[128,4096]{1,0:T(8,128)(2,1)S(1)}, u32[]{:S(2)}) copy-start(bf16[128,4096]{1,0:T(8,128)(2,1)S(1)} %collective-permute-done) | copy-start | bytes 3145732
  128.2 70.7 %collective-permute-start.5 = (bf16[128,4096]{1,0:T(8,128)(2,1)}, bf16[128,4096]{1,0:T(8,128)(2,1)}, u32[]{:S(2)}, u32[]{:S(2)}) collective-permute-start(bf16[128,4096]{1,0:T(8,128)(2,1)} %get-tuple-element.26), channel_id=1, source_target_pairs={{0,96},{4,100},{8,104},{12,108},{16,112},{20,116},{24,120},{28,124... | collective-permute-start | bytes 3145736 | tf_op jit(solution)/shard_map/ppermute | solution.py:14
  158.2 20.5 %copy-start.4 = (bf16[128,4096]{1,0:T(8,128)(2,1)}, bf16[128,4096]{1,0:T(8,128)(2,1)S(1)}, u32[]{:S(2)}) copy-start(bf16[128,4096]{1,0:T(8,128)(2,1)S(1)} %collective-permute-done.1) | copy-start | bytes 3145732
  158.2 52.1 %collective-permute-start.6 = (bf16[128,4096]{1,0:T(8,128)(2,1)S(1)}, bf16[128,4096]{1,0:T(8,128)(2,1)}, u32[]{:S(2)}, u32[]{:S(2)}) collective-permute-start(bf16[128,4096]{1,0:T(8,128)(2,1)S(1)} %get-tuple-element.25), channel_id=1, source_target_pairs={{0,112},{4,116},{8,120},{12,124},{1,113},{5,117},{9,121},{13,125},... | collective-permute-start | bytes 3145736 | tf_op jit(solution)/shard_map/ppermute | solution.py:14
  216.1 21.3 %collective-permute-start.7 = (bf16[128,4096]{1,0:T(8,128)(2,1)S(1)}, bf16[128,4096]{1,0:T(8,128)(2,1)S(1)}, u32[]{:S(2)}, u32[]{:S(2)}) collective-permute-start(bf16[128,4096]{1,0:T(8,128)(2,1)S(1)} %add_convert_fusion), channel_id=1, source_target_pairs={{124,0},{0,4},{4,8},{8,12},{12,16},{16,20},{20,24},{24,28},{28,32}... | collective-permute-start | bytes 3145736 | tf_op jit(solution)/shard_map/ppermute | solution.py:20
Sparse Core Ops, SparseCore 0:
  10.8 50.6 all-gather.1
  95.5 47.1 reduce-scatter.1
where the time goes:
time: 246 us; the launch traced here: 245 us
  waiting for transfers between devices  107 us (43%)
  starting transfers between devices  68.9 us (28%)
  matrix products  33.5 us (14%)
  between operations  17.8 us (7%)
  other arithmetic  10.1 us (4%)
  local copies, waits for them, and re-layouts  7.55 us (3%)
    ppermute x7, starting transfers between devices, passed_along(): lax.ppermute(value, axis, [(source, source + steps) for source in range(f...  68.8 us
    all_gather x1, waiting for transfers between devices, on_device(): row_piece = lax.all_gather(normed, 'tensor', axis=0, tiled=True)  50.7 us
    ppermute x7, waiting for transfers between devices, passed_along(): lax.ppermute(value, axis, [(source, source + steps) for source in range(f...  35.4 us
    ppermute x1, waiting for transfers between devices, from_behind(): return lax.ppermute(block, axis, route)  21.2 us
    dot_general x1, matrix products, on_device(): jnp.dot(row_piece, query_local, preferred_element_type=jnp.float32)  7.47 us
    sub x1, matrix products, attend(): softmax_weights = jax.nn.softmax(scores, axis=-1).astype(jnp.bfloat16)  7.28 us
    dot_general x1, matrix products, attend(): jnp.einsum('gjts,sgd->tgjd', softmax_weights, value_rows, preferred_eleme...  5.99 us
    convert_element_type x1, other arithmetic, on_device(): (self_coefficient[0] * block_out.astype(jnp.float32) + history_sum).astyp...  5.81 us
  transfers between devices with their start and end apart: 10, of which 5 were waited for; matrix products, arithmetic and copies ran while one was open for 3% of the time, Pallas kernels for 0%

commit v1 on v0

--- a/solution.py
+++ b/solution.py
@@ -67,7 +67,14 @@
     query_local = query_weight[0]
     key_local = key_weight[0]
     value_local = value_weight[0]
-    row_piece = lax.all_gather(normed, "tensor", axis=0, tiled=True)
+    ring = [normed]
+    for hop in range(3):
+        ring.append(lax.ppermute(ring[-1], "tensor", [(dev, (dev + 1) % 4) for dev in range(4)]))
+    row_piece = jnp.roll(
+        jnp.concatenate(ring[::-1], axis=0),
+        (lax.axis_index("tensor") + 1) * ring[0].shape[0],
+        axis=0,
+    )
     query_part = jnp.dot(row_piece, query_local, preferred_element_type=jnp.float32).astype(
         jnp.bfloat16
     )

time: 246 us -> 278 us (1.13)
  waiting for transfers between devices: 107 us -> 130 us
  local copies, waits for them, and re-layouts: 7.55 us -> 18.1 us
    ppermute x0 -> x3, waiting for transfers between devices: none -> 73.8 us  [on_device(): lax.ppermute(ring[-1], 'tensor', [(dev, (dev + 1) % 4) for dev in range(4)])]
    all_gather x1 -> x0, waiting for transfers between devices: 50.7 us -> none  [on_device(): row_piece = lax.all_gather(normed, 'tensor', axis=0, tiled=True)]
    unnamed x17 -> x27, local copies, waits for them, and re-layouts: 1.01 us -> 10.9 us
    ppermute x7, waiting for transfers between devices: 35.4 us -> 31.9 us  [passed_along(): lax.ppermute(value, axis, [(source, source + steps) for source in range(f...]
    ppermute x1, waiting for transfers between devices: 21.2 us -> 24.5 us  [from_behind(): return lax.ppermute(block, axis, route)]
    dot_general x1, matrix products: 7.47 us -> 4.28 us  [on_device(): jnp.dot(row_piece, query_local, preferred_element_type=jnp.float32)]
    ppermute x7, starting transfers between devices: 68.8 us -> 65.9 us  [passed_along(): lax.ppermute(value, axis, [(source, source + steps) for source in range(f...]
  transfers between devices with their start and end apart: 10 -> 12, of which waited for: 5 -> 7; matrix products, arithmetic and copies ran while one was open for 3% -> 2% of each run, Pallas kernels for 0% -> 0%
where the time goes in v1:
time: 278 us; the launch traced here: 277 us
  waiting for transfers between devices  130 us (47%)
  starting transfers between devices  68.1 us (24%)
  matrix products  32.6 us (12%)
  local copies, waits for them, and re-layouts  18.1 us (7%)
  between operations  18.1 us (7%)
  other arithmetic  9.88 us (4%)
    ppermute x3, waiting for transfers between devices, on_device(): lax.ppermute(ring[-1], 'tensor', [(dev, (dev + 1) % 4) for dev in range(4)])  73.8 us
    ppermute x7, starting transfers between devices, passed_along(): lax.ppermute(value, axis, [(source, source + steps) for source in range(f...  65.9 us
    ppermute x7, waiting for transfers between devices, passed_along(): lax.ppermute(value, axis, [(source, source + steps) for source in range(f...  31.9 us
    ppermute x1, waiting for transfers between devices, from_behind(): return lax.ppermute(block, axis, route)  24.5 us
    unnamed x27, local copies, waits for them, and re-layouts  10.9 us
    dot_general x1, matrix products, on_device(): jnp.dot(row_piece, output_local, preferred_element_type=jnp.float32)  7.81 us
    sub x1, matrix products, attend(): softmax_weights = jax.nn.softmax(scores, axis=-1).astype(jnp.bfloat16)  7.28 us
    convert_element_type x1, other arithmetic, on_device(): (self_coefficient[0] * block_out.astype(jnp.float32) + history_sum).astyp...  6.01 us
  transfers between devices with their start and end apart: 12, of which 7 were waited for; matrix products, arithmetic and copies ran while one was open for 2% of the time, Pallas kernels for 0%

profile of v1, /device:TPU:0, one launch (start us, length us, event | category | flops | bytes accessed | tf_op | source)
XLA Modules:
  0.0 277.1 jit_solution(2245456512638156961)
XLA Ops:
  9.7 1.7 collective-permute-start
  11.4 24.4 %collective-permute-done = bf16[128,4096]{1,0:T(8,128)(2,1)S(1)} collective-permute-done((bf16[128,4096]{1,0:T(8,128)(2,1)S(1)}, bf16[128,4096]{1,0:T(8,128)(2,1)S(1)}, u32[]{:S(2)}, u32[]{:S(2)}) %collective-permute-start) | collective-permute-done | bytes 1048608 | tf_op jit(solution)/shard_map/ppermute | solution.py:72
  36.3 24.8 %collective-permute-done.1 = bf16[128,4096]{1,0:T(8,128)(2,1)} collective-permute-done((bf16[128,4096]{1,0:T(8,128)(2,1)S(1)}, bf16[128,4096]{1,0:T(8,128)(2,1)}, u32[]{:S(2)}, u32[]{:S(2)}) %collective-permute-start.1) | collective-permute-done | bytes 1048608 | tf_op jit(solution)/shard_map/ppermute | solution.py:72
  61.2 24.5 %collective-permute-done.2 = bf16[128,4096]{1,0:T(8,128)(2,1)} collective-permute-done((bf16[128,4096]{1,0:T(8,128)(2,1)}, bf16[128,4096]{1,0:T(8,128)(2,1)}, u32[]{:S(2)}, u32[]{:S(2)}) %collective-permute-start.2) | collective-permute-done | bytes 1048608 | tf_op jit(solution)/shard_map/ppermute | solution.py:72
  92.0 3.2 %copy-done.5 = bf16[1024,4096]{1,0:T(8,128)(2,1)} copy-done((bf16[1024,4096]{1,0:T(8,128)(2,1)}, bf16[1024,4096]{1,0:T(8,128)(2,1)S(1)}, u32[]{:S(2)}) %copy-start.5) | copy-done | bytes 8388632
  95.2 4.3 %fusion.24 = bf16[512,768]{1,0:T(8,128)(2,1)} fusion(bf16[1,4096,768]{2,1,0:T(8,128)(2,1)S(1)} %bitcast.82, bf16[1024,4096]{1,0:T(8,128)(2,1)S(1)} %constant_dynamic-update-slice_fusion, s32[]{:T(128)S(6)} %select_n.41), kind=kOutput, calls=%fused_computation.28 | convolution fusion | flops 3221618688 | bytes 11272196 | tf_op jit(solution)/shard_map/dot_general | solution.py:78
  101.0 3.8 %fusion.32 = bf16[512,128]{0,1:T(8,128)(2,1)S(1)} fusion(bf16[1024,4096]{1,0:T(8,128)(2,1)} %copy-done.5, s32[]{:T(128)S(6)} %select_n.41, bf16[1,4096,128]{2,1,0:T(8,128)(2,1)S(1)} %copy-done), kind=kOutput, calls=%fused_computation.30 | convolution fusion | flops 536936448 | bytes 5373956 | tf_op jit(solution)/shard_map/dot_general | solution.py:81
  104.8 3.7 %fusion.29 = bf16[512,128]{0,1:T(8,128)(2,1)S(1)} fusion(bf16[1024,4096]{1,0:T(8,128)(2,1)} %copy-done.5, s32[]{:T(128)S(6)} %select_n.41, bf16[1,4096,128]{2,1,0:T(8,128)(2,1)S(1)} %copy-done.7), kind=kOutput, calls=%fused_computation.29 | convolution fusion | flops 536936448 | bytes 5373956 | tf_op jit(solution)/shard_map/dot_general | solution.py:84
  108.5 7.3 %fusion.43 = (f32[2,6,512]{2,1,0:T(8,128)S(1)}, f32[2,6,512,512]{2,3,1,0:T(8,128)}) fusion(pred[512,512]{0,1:T(8,128)(4,1)S(1)} %iota_compare_fusion, bf16[512,2,64,1]{0,2,3,1:T(8,128)(2,1)S(1)} %bitcast.85, bf16[512,2,6,64]{0,3,2,1:T(8,128)(2,1)S(1)} %bitcast.80), kind=kOutput, calls=%fused_computation.58 | convolution fusion | flops 415236608 | bytes 13787136 | tf_op jit(solution)/shard_map/while/body/eval_jaxpr/sub | solution.py:41
  115.8 5.8 %fusion.23 = bf16[2,64,6,512]{3,1,2,0:T(8,128)(2,1)S(1)} fusion(bf16[512,2,64,1]{0,2,3,1:T(8,128)(2,1)S(1)} %bitcast.84, f32[2,6,512,512]{2,3,1,0:T(8,128)} %get-tuple-element.36, f32[2,6,512]{2,1,0:T(8,128)S(1)} %get-tuple-element.35), kind=kOutput, calls=%fused_computation.27 | convolution fusion | flops 409337856 | bytes 13524992 | tf_op jit(solution)/shard_map/while/body/eval_jaxpr/gjts,sgd->tgjd/dot_general | solution.py:42
  121.5 7.8 %fusion.10 = bf16[512,4096]{1,0:T(8,128)(2,1)} fusion(bf16[512,768]{0,1:T(8,128)(2,1)S(1)} %bitcast.83, bf16[1,768,4096]{2,1,0:T(8,128)(2,1)} %param.12), kind=kOutput, calls=%fused_computation.13 | convolution fusion | flops 3223322624 | bytes 11272192 | tf_op jit(solution)/shard_map/dot_general | solution.py:106
  129.4 5.1 %slice_bitcast_fusion.6 = (bf16[128,4096]{1,0:T(8,128)(2,1)S(1)}, bf16[128,4096]{1,0:T(8,128)(2,1)}, bf16[128,4096]{1,0:T(8,128)(2,1)}, bf16[128,4096]{1,0:T(8,1...) fusion(bf16[1,7,128,4096]{3,2,1,0:T(8,128)(2,1)} %param.8), kind=kLoop, calls=%fused_computation.39 | loop fusion | bytes 14680064 | tf_op jit(solution)/shard_map/squeeze | solution.py:58
  134.5 6.2 %collective-permute-start.3 = (bf16[128,4096]{1,0:T(8,128)(2,1)S(1)}, bf16[128,4096]{1,0:T(8,128)(2,1)S(1)}, u32[]{:S(2)}, u32[]{:S(2)}) collective-permute-start(bf16[128,4096]{1,0:T(8,128)(2,1)S(1)} %get-tuple-element.13), channel_id=1, source_target_pairs={{0,16},{4,20},{8,24},{12,28},{16,32},{20,36},{24,40},{28,44},{32,4... | collective-permute-start | bytes 3145736 | tf_op jit(solution)/shard_map/ppermute | solution.py:14
  140.7 3.5 %collective-permute-start.4 = (bf16[128,4096]{1,0:T(8,128)(2,1)S(1)}, bf16[128,4096]{1,0:T(8,128)(2,1)S(1)}, u32[]{:S(2)}, u32[]{:S(2)}) collective-permute-start(bf16[128,4096]{1,0:T(8,128)(2,1)S(1)} %get-tuple-element.24), channel_id=1, source_target_pairs={{0,32},{4,36},{8,40},{12,44},{16,48},{20,52},{24,56},{28,60},{32,6... | collective-permute-start | bytes 3145736 | tf_op jit(solution)/shard_map/ppermute | solution.py:14
  144.2 4.2 %collective-permute-start.5 = (bf16[128,4096]{1,0:T(8,128)(2,1)}, bf16[128,4096]{1,0:T(8,128)(2,1)}, u32[]{:S(2)}, u32[]{:S(2)}) collective-permute-start(bf16[128,4096]{1,0:T(8,128)(2,1)} %get-tuple-element.22), channel_id=1, source_target_pairs={{0,48},{4,52},{8,56},{12,60},{16,64},{20,68},{24,72},{28,76},{32,8... | collective-permute-start | bytes 3145736 | tf_op jit(solution)/shard_map/ppermute | solution.py:14
  148.4 3.5 %collective-permute-start.6 = (bf16[128,4096]{1,0:T(8,128)(2,1)}, bf16[128,4096]{1,0:T(8,128)(2,1)}, u32[]{:S(2)}, u32[]{:S(2)}) collective-permute-start(bf16[128,4096]{1,0:T(8,128)(2,1)} %get-tuple-element.20), channel_id=1, source_target_pairs={{0,64},{4,68},{8,72},{12,76},{16,80},{20,84},{24,88},{28,92},{32,9... | collective-permute-start | bytes 3145736 | tf_op jit(solution)/shard_map/ppermute | solution.py:14
  152.0 2.3 collective-permute-start.7
  154.3 6.2 %collective-permute-done.3 = bf16[128,4096]{1,0:T(8,128)(2,1)S(1)} collective-permute-done((bf16[128,4096]{1,0:T(8,128)(2,1)S(1)}, bf16[128,4096]{1,0:T(8,128)(2,1)S(1)}, u32[]{:S(2)}, u32[]{:S(2)}) %collective-permute-start.3) | collective-permute-done | bytes 1048608 | tf_op jit(solution)/shard_map/ppermute | solution.py:14
  160.5 28.5 %collective-permute-start.8 = (bf16[128,4096]{1,0:T(8,128)(2,1)S(1)}, bf16[128,4096]{1,0:T(8,128)(2,1)}, u32[]{:S(2)}, u32[]{:S(2)}) collective-permute-start(bf16[128,4096]{1,0:T(8,128)(2,1)S(1)} %get-tuple-element.26), channel_id=1, source_target_pairs={{0,96},{4,100},{8,104},{12,108},{16,112},{20,116},{24,120},{28,124... | collective-permute-start | bytes 3145736 | tf_op jit(solution)/shard_map/ppermute | solution.py:14
  190.0 17.7 %collective-permute-start.9 = (bf16[128,4096]{1,0:T(8,128)(2,1)S(1)}, bf16[128,4096]{1,0:T(8,128)(2,1)}, u32[]{:S(2)}, u32[]{:S(2)}) collective-permute-start(bf16[128,4096]{1,0:T(8,128)(2,1)S(1)} %get-tuple-element.25), channel_id=1, source_target_pairs={{0,112},{4,116},{8,120},{12,124},{1,113},{5,117},{9,121},{13,125},... | collective-permute-start | bytes 3145736 | tf_op jit(solution)/shard_map/ppermute | solution.py:14
  213.0 18.4 %collective-permute-done.7 = bf16[128,4096]{1,0:T(8,128)(2,1)} collective-permute-done((bf16[128,4096]{1,0:T(8,128)(2,1)}, bf16[128,4096]{1,0:T(8,128)(2,1)}, u32[]{:S(2)}, u32[]{:S(2)}) %collective-permute-start.7) | collective-permute-done | bytes 1048608 | tf_op jit(solution)/shard_map/ppermute | solution.py:14
  231.3 7.3 %collective-permute-done.9 = bf16[128,4096]{1,0:T(8,128)(2,1)} collective-permute-done((bf16[128,4096]{1,0:T(8,128)(2,1)S(1)}, bf16[128,4096]{1,0:T(8,128)(2,1)}, u32[]{:S(2)}, u32[]{:S(2)}) %collective-permute-start.9) | collective-permute-done | bytes 1048608 | tf_op jit(solution)/shard_map/ppermute | solution.py:14
  238.6 6.0 %add_convert_fusion = bf16[128,4096]{1,0:T(8,128)(2,1)S(1)} fusion(bf16[128,4096]{1,0:T(8,128)(2,1)} %collective-permute-done.9, bf16[128,4096]{1,0:T(8,128)(2,1)} %collective-permute-done.8, bf16[128,4096]{1,0:T(8,128)(2,1)} %collective-permute-done.7, bf16[128,4096]{1,0:T(8,128)(2,1)} %collective-permute-done.6, ...), kind=kLoop, calls=%fused_computation.25 | loop fusion | flops 14680064 | bytes 10485792 | tf_op jit(solution)/shard_map/convert_element_type | solution.py:116
  244.7 24.5 %collective-permute-done.10 = bf16[128,4096]{1,0:T(8,128)(2,1)S(1)} collective-permute-done((bf16[128,4096]{1,0:T(8,128)(2,1)S(1)}, bf16[128,4096]{1,0:T(8,128)(2,1)S(1)}, u32[]{:S(2)}, u32[]{:S(2)}) %collective-permute-start.10) | collective-permute-done | bytes 1048608 | tf_op jit(solution)/shard_map/ppermute | solution.py:20
  (47 shorter events, 14.2 us)
Async XLA Ops:
  6.5 94.4 %copy-start = (bf16[1,4096,128]{2,1,0:T(8,128)(2,1)S(1)}, bf16[1,4096,128]{2,1,0:T(8,128)(2,1)}, u32[]{:S(2)}) copy-start(bf16[1,4096,128]{2,1,0:T(8,128)(2,1)} %param.10) | copy-start | bytes 3145732
  6.5 82.1 %copy-start.2 = (bf16[1,128,4096]{2,1,0:T(8,128)(2,1)S(1)}, bf16[1,128,4096]{2,1,0:T(8,128)(2,1)}, u32[]{:S(2)}) copy-start(bf16[1,128,4096]{2,1,0:T(8,128)(2,1)} %param.7) | copy-start | bytes 3145732
  6.5 232.1 %reduce-scatter.2.cloned.1.call-start = ((), (), s32[]{:S(2)}) async-start(), calls=%async_computation.1 | async-start | bytes 5242880 | tf_op jit(solution)/shard_map/reduce_scatter | solution.py:109
  9.7 26.1 %collective-permute-start = (bf16[128,4096]{1,0:T(8,128)(2,1)S(1)}, bf16[128,4096]{1,0:T(8,128)(2,1)S(1)}, u32[]{:S(2)}, u32[]{:S(2)}) collective-permute-start(bf16[128,4096]{1,0:T(8,128)(2,1)S(1)} %fusion.19), channel_id=1, source_target_pairs={{0,1},{1,2},{2,3},{3,0},{4,5},{5,6},{6,7},{7,4},{8,9},{9,10},{10,1... | collective-permute-start | bytes 3145736 | tf_op jit(solution)/shard_map/ppermute | solution.py:72
  35.8 25.3 %collective-permute-start.1 = (bf16[128,4096]{1,0:T(8,128)(2,1)S(1)}, bf16[128,4096]{1,0:T(8,128)(2,1)}, u32[]{:S(2)}, u32[]{:S(2)}) collective-permute-start(bf16[128,4096]{1,0:T(8,128)(2,1)S(1)} %collective-permute-done), channel_id=1, source_target_pairs={{0,1},{1,2},{2,3},{3,0},{4,5},{5,6},{6,7},{7,4},{8,9},{9,10},{10,1... | collective-permute-start | bytes 3145736 | tf_op jit(solution)/shard_map/ppermute | solution.py:72
  61.1 24.6 %collective-permute-start.2 = (bf16[128,4096]{1,0:T(8,128)(2,1)}, bf16[128,4096]{1,0:T(8,128)(2,1)}, u32[]{:S(2)}, u32[]{:S(2)}) collective-permute-start(bf16[128,4096]{1,0:T(8,128)(2,1)} %collective-permute-done.1), channel_id=1, source_target_pairs={{0,1},{1,2},{2,3},{3,0},{4,5},{5,6},{6,7},{7,4},{8,9},{9,10},{10,1... | collective-permute-start | bytes 3145736 | tf_op jit(solution)/shard_map/ppermute | solution.py:72
  87.0 8.2 %slice-start = ((s8[6291456]{0:T(1024)(128)(4,1)}), s8[4194304]{0:T(1024)(128)(4,1)S(1)}, s32[]{:S(2)}) async-start(s8[6291456]{0:T(1024)(128)(4,1)} %bitcast.81), calls=%async_computation.2 | async-start | bytes 8388608
  88.9 6.4 %slice-start.1 = ((s8[6291456]{0:T(1024)(128)(4,1)}), s8[2097152]{0:T(1024)(128)(4,1)S(1)}, s32[]{:S(2)}) async-start(s8[6291456]{0:T(1024)(128)(4,1)} %bitcast.81), calls=%async_computation.3 | async-start | bytes 4194304
  92.0 3.2 %copy-start.5 = (bf16[1024,4096]{1,0:T(8,128)(2,1)}, bf16[1024,4096]{1,0:T(8,128)(2,1)S(1)}, u32[]{:S(2)}) copy-start(bf16[1024,4096]{1,0:T(8,128)(2,1)S(1)} %constant_dynamic-update-slice_fusion) | copy-start | bytes 25165828
  100.9 3.8 %copy-start.7 = (bf16[1,4096,128]{2,1,0:T(8,128)(2,1)S(1)}, bf16[1,4096,128]{2,1,0:T(8,128)(2,1)}, u32[]{:S(2)}) copy-start(bf16[1,4096,128]{2,1,0:T(8,128)(2,1)} %param.11) | copy-start | bytes 3145732
  129.4 78.3 %copy-start.6 = (f32[32,8]{0,1:T(8,128)S(1)}, f32[32,8]{0,1:T(8,128)}, u32[]{:S(2)}) copy-start(f32[32,8]{0,1:T(8,128)} %param.13) | copy-start | bytes 3076
  134.5 26.0 %collective-permute-start.3 = (bf16[128,4096]{1,0:T(8,128)(2,1)S(1)}, bf16[128,4096]{1,0:T(8,128)(2,1)S(1)}, u32[]{:S(2)}, u32[]{:S(2)}) collective-permute-start(bf16[128,4096]{1,0:T(8,128)(2,1)S(1)} %get-tuple-element.13), channel_id=1, source_target_pairs={{0,16},{4,20},{8,24},{12,28},{16,32},{20,36},{24,40},{28,44},{32,4... | collective-permute-start | bytes 3145736 | tf_op jit(solution)/shard_map/ppermute | solution.py:14
  140.7 48.2 %collective-permute-start.4 = (bf16[128,4096]{1,0:T(8,128)(2,1)S(1)}, bf16[128,4096]{1,0:T(8,128)(2,1)S(1)}, u32[]{:S(2)}, u32[]{:S(2)}) collective-permute-start(bf16[128,4096]{1,0:T(8,128)(2,1)S(1)} %get-tuple-element.24), channel_id=1, source_target_pairs={{0,32},{4,36},{8,40},{12,44},{16,48},{20,52},{24,56},{28,60},{32,6... | collective-permute-start | bytes 3145736 | tf_op jit(solution)/shard_map/ppermute | solution.py:14
  144.2 68.7 %collective-permute-start.5 = (bf16[128,4096]{1,0:T(8,128)(2,1)}, bf16[128,4096]{1,0:T(8,128)(2,1)}, u32[]{:S(2)}, u32[]{:S(2)}) collective-permute-start(bf16[128,4096]{1,0:T(8,128)(2,1)} %get-tuple-element.22), channel_id=1, source_target_pairs={{0,48},{4,52},{8,56},{12,60},{16,64},{20,68},{24,72},{28,76},{32,8... | collective-permute-start | bytes 3145736 | tf_op jit(solution)/shard_map/ppermute | solution.py:14
  148.4 64.5 %collective-permute-start.6 = (bf16[128,4096]{1,0:T(8,128)(2,1)}, bf16[128,4096]{1,0:T(8,128)(2,1)}, u32[]{:S(2)}, u32[]{:S(2)}) collective-permute-start(bf16[128,4096]{1,0:T(8,128)(2,1)} %get-tuple-element.20), channel_id=1, source_target_pairs={{0,64},{4,68},{8,72},{12,76},{16,80},{20,84},{24,88},{28,92},{32,9... | collective-permute-start | bytes 3145736 | tf_op jit(solution)/shard_map/ppermute | solution.py:14
  152.0 79.4 %collective-permute-start.7 = (bf16[128,4096]{1,0:T(8,128)(2,1)}, bf16[128,4096]{1,0:T(8,128)(2,1)}, u32[]{:S(2)}, u32[]{:S(2)}) collective-permute-start(bf16[128,4096]{1,0:T(8,128)(2,1)} %get-tuple-element.14), channel_id=1, source_target_pairs={{0,80},{4,84},{8,88},{12,92},{16,96},{20,100},{24,104},{28,108},{3... | collective-permute-start | bytes 3145736 | tf_op jit(solution)/shard_map/ppermute | solution.py:14
  160.5 28.5 %copy-start.3 = (bf16[128,4096]{1,0:T(8,128)(2,1)}, bf16[128,4096]{1,0:T(8,128)(2,1)S(1)}, u32[]{:S(2)}) copy-start(bf16[128,4096]{1,0:T(8,128)(2,1)S(1)} %collective-permute-done.3) | copy-start | bytes 3145732
  160.5 70.8 %collective-permute-start.8 = (bf16[128,4096]{1,0:T(8,128)(2,1)S(1)}, bf16[128,4096]{1,0:T(8,128)(2,1)}, u32[]{:S(2)}, u32[]{:S(2)}) collective-permute-start(bf16[128,4096]{1,0:T(8,128)(2,1)S(1)} %get-tuple-element.26), channel_id=1, source_target_pairs={{0,96},{4,100},{8,104},{12,108},{16,112},{20,116},{24,120},{28,124... | collective-permute-start | bytes 3145736 | tf_op jit(solution)/shard_map/ppermute | solution.py:14
  189.0 1.0 copy-start.4
  190.0 48.6 %collective-permute-start.9 = (bf16[128,4096]{1,0:T(8,128)(2,1)S(1)}, bf16[128,4096]{1,0:T(8,128)(2,1)}, u32[]{:S(2)}, u32[]{:S(2)}) collective-permute-start(bf16[128,4096]{1,0:T(8,128)(2,1)S(1)} %get-tuple-element.25), channel_id=1, source_target_pairs={{0,112},{4,116},{8,120},{12,124},{1,113},{5,117},{9,121},{13,125},... | collective-permute-start | bytes 3145736 | tf_op jit(solution)/shard_map/ppermute | solution.py:14
  238.6 31.6 %copy-start.1 = (bf16[1,4096,128]{2,1,0:T(8,128)(2,1)S(1)}, bf16[1,4096,128]{2,1,0:T(8,128)(2,1)}, u32[]{:S(2)}) copy-start(bf16[1,4096,128]{2,1,0:T(8,128)(2,1)} %param.10) | copy-start | bytes 3145732
  244.6 24.6 %collective-permute-start.10 = (bf16[128,4096]{1,0:T(8,128)(2,1)S(1)}, bf16[128,4096]{1,0:T(8,128)(2,1)S(1)}, u32[]{:S(2)}, u32[]{:S(2)}) collective-permute-start(bf16[128,4096]{1,0:T(8,128)(2,1)S(1)} %add_convert_fusion), channel_id=1, source_target_pairs={{124,0},{0,4},{4,8},{8,12},{12,16},{16,20},{20,24},{24,28},{28,32}... | collective-permute-start | bytes 3145736 | tf_op jit(solution)/shard_map/ppermute | solution.py:20
Sparse Core Ops, SparseCore 0:
  129.5 47.0 reduce-scatter.1
